TPU v7x, 32 devices: a whole 2x2x4 slice. The times are simulated.
32 devices in a mesh: group: 2 (over y), tm: 4 (over z), bl: 2 (over x), pol: 2 (over core).
Axes of the slice: x: 2, y: 2, z: 4, core: 2. Of those that a mesh axis runs over, the one named last changes fastest.
Arguments:
- visibilities: bfloat16 [1600, 256, 2, 384], P(('group', 'tm'), ('bl', 'pol')), parts along dimension 0, may hold values from -6 to 6
- flag_mask: int32 [1600], P(('group', 'tm')), parts along dimension 0, may hold values 0 or 1
- kernel_index: int32 [256], P(('bl', 'pol')), may hold values from 0 to 15
- filter_bank: float32 [2, 16, 257], replicated, may hold values from -0.875 to 0.875
Outputs:
- fringe_filtered: bfloat16 [160, 256, 2, 384], P('group', ('bl', 'pol', 'tm')), parts along dimension 0
There are 2 independent parts, one for each index of `group`. A program takes and returns all parts, laid end to end along the dimension named above; an argument that names none is the same for every part. Nothing has to cross between parts.
All inputs are finite; a program needn't handle non-finite values. No bound on the sum of `flag_mask` on one device may be relied on, other than what follows from the above.
Results may differ from a plain program's by a relative error of at most 0.001.
Values may be sent and summed in bfloat16 or wider, within the bound.
A program may use at most 192 MiB of HBM per device.

v0:
```python
import jax
import jax.numpy as jnp
from jax import lax
from jax.sharding import PartitionSpec as P

TAPS = 257
AVG = 10


def padded(block, sides, width):
    for axis, dim in sides:
        count = lax.axis_size(axis)
        forward = [(i, i + 1) for i in range(count - 1)]
        backward = [(target, source) for source, target in forward]
        low = lax.ppermute(
            lax.slice_in_dim(block, block.shape[dim] - width, None, axis=dim), axis, forward
        )
        high = lax.ppermute(lax.slice_in_dim(block, 0, width, axis=dim), axis, backward)
        block = jnp.concatenate([low, block, high], axis=dim)
    return block


def select_taps(kernel_index, filter_bank):
    choices_count = filter_bank.shape[1]
    one_hot = (kernel_index[:, None] == jnp.arange(choices_count, dtype=jnp.int32)[None, :]).astype(
        jnp.float32
    )
    return jnp.einsum("bk,rkt->brt", one_hot, filter_bank, precision=lax.Precision.HIGHEST)


def make_band(kernel_taps, block_rows):
    tap_count = kernel_taps.shape[1]
    row_width = block_rows + tap_count - 1
    zero_tail = jnp.zeros((2, block_rows), jnp.float32)
    period_row = jnp.concatenate([kernel_taps, zero_tail], axis=1)
    tiled_rows = jnp.tile(period_row, (1, block_rows))[:, : block_rows * row_width]
    return tiled_rows.reshape(2, block_rows, row_width)


def filter_block(time_slab, kernel_taps, block_rows):
    band_rows = make_band(kernel_taps, block_rows)
    row_width = band_rows.shape[2]
    band_rows = band_rows.reshape(2, block_rows // AVG, AVG, row_width).sum(axis=2) * (1.0 / AVG)
    out_count = band_rows.shape[1]
    stacked = band_rows.reshape(2 * out_count, row_width)
    product = jnp.dot(
        stacked, time_slab, precision=lax.Precision.HIGHEST, preferred_element_type=jnp.float32
    )
    prod_real = product[:out_count]
    prod_imag = product[out_count:]
    channels = time_slab.shape[1] // 2
    out_real = prod_real[:, :channels] - prod_imag[:, channels:]
    out_imag = prod_real[:, channels:] + prod_imag[:, :channels]
    result = jnp.stack([out_real, out_imag], axis=1)
    return result


def per_device(visibilities, flag_mask, kernel_index, filter_bank):
    half_taps = TAPS // 2
    block_rows = visibilities.shape[0]
    masked = visibilities * flag_mask.astype(jnp.bfloat16)[:, None, None, None]
    extended = padded(masked, (("tm", 0),), half_taps)
    taps_all = select_taps(kernel_index, filter_bank)

    def per_base(base_index):
        time_slab = lax.dynamic_index_in_dim(extended, base_index, 1, False).astype(jnp.float32)
        time_slab = time_slab.reshape(extended.shape[0], -1)
        kernel_taps = lax.dynamic_index_in_dim(taps_all, base_index, 0, False)
        return filter_block(time_slab, kernel_taps, block_rows)

    filtered = lax.map(per_base, jnp.arange(visibilities.shape[1], dtype=jnp.int32))
    averaged = jnp.moveaxis(filtered, 0, 1).astype(jnp.bfloat16)
    return lax.all_to_all(averaged, "tm", split_axis=1, concat_axis=0, tiled=True)


def solution(mesh):
    placed = (
        P(("group", "tm"), ("bl", "pol"), None, None),
        P(("group", "tm")),
        P(("bl", "pol")),
        P(),
    )
    return jax.shard_map(
        per_device,
        mesh=mesh,
        in_specs=placed,
        out_specs=P("group", ("bl", "pol", "tm"), None, None),
        check_vma=False,
    )
```

profile of v0, /device:TPU:10, one launch (start us, length us, event | category | flops | bytes accessed | tf_op | source)
XLA Modules:
  0.0 982.3 jit_solution(15027337351065907888)
XLA Ops:
  0.7 25.5 %broadcast_multiply_fusion.1 = bf16[200,64,2,384]{3,2,1,0:T(2,128)(2,1)S(1)} fusion(bf16[200,64,2,384]{3,2,1,0:T(2,128)(2,1)} %param.6, bf16[200]{0:T(256)(128)(2,1)S(1)} %convert_element_type.11), kind=kLoop, calls=%fused_computation.11 | loop fusion | flops 9830400 | bytes 39322000 | tf_op jit(solution)/shard_map/mul | solution.py:61
  26.2 23.1 %fusion.6 = (bf16[128,64,2,384]{3,2,1,0:T(2,128)(2,1)}, bf16[128,64,2,384]{3,2,1,0:T(2,128)(2,1)}) fusion(bf16[200,64,2,384]{3,2,1,0:T(2,128)(2,1)S(1)} %broadcast_multiply_fusion.1), kind=kLoop, calls=%fused_computation.17 | loop fusion | bytes 50331648 | tf_op jit(solution)/shard_map/slice | solution.py:16
  49.3 3.5 collective-permute-start
  52.8 6.9 collective-permute-start.1
  60.0 263.6 %collective-permute-done = bf16[128,64,2,384]{3,2,1,0:T(2,128)(2,1)} collective-permute-done((bf16[128,64,2,384]{3,2,1,0:T(2,128)(2,1)}, bf16[128,64,2,384]{3,2,1,0:T(2,128)(2,1)}, u32[]{:S(2)}, u32[]{:S(2)}) %collective-permute-start) | collective-permute-done | bytes 12582944 | tf_op jit(solution)/shard_map/ppermute | solution.py:15
  323.6 5.7 collective-permute-done.1
  329.3 69.3 %pad_maximum_fusion = bf16[456,64,2,384]{3,2,1,0:T(2,128)(2,1)} fusion(bf16[128,64,2,384]{3,2,1,0:T(2,128)(2,1)} %collective-permute-done.1, bf16[200,64,2,384]{3,2,1,0:T(2,128)(2,1)} %copy-done.2, bf16[128,64,2,384]{3,2,1,0:T(2,128)(2,1)} %collective-permute-done), kind=kLoop, calls=%fused_computation.10 | loop fusion | flops 44826624 | bytes 89653248 | tf_op jit(solution)/shard_map/concatenate | solution.py:19
  398.7 532.0 %while.10 = (s32[]{:T(128)}, bf16[64,20,2,384]{3,2,1,0:T(2,128)(2,1)}, s32[64]{0:T(128)S(1)}, f32[64,2,257]{2,0,1:T(8,128)S(1)}, bf16[456,64,2,384]{3,2,1,0:T(2,...) while((s32[]{:T(128)}, bf16[64,20,2,384]{3,2,1,0:T(2,128)(2,1)}, s32[64]{0:T(128)S(1)}, ...), condition=%wide.region_2.3_spmd, body=%wide.region_0.2_spmd.sunk | while | flops 168328320 | bytes 10199059 | solution.py:71
  404.1 1.6 constant_dynamic-slice_fusion.5
  412.5 1.6 constant_dynamic-slice_fusion.5
  420.8 1.6 constant_dynamic-slice_fusion.5
  429.1 1.6 constant_dynamic-slice_fusion.5
  437.4 1.6 constant_dynamic-slice_fusion.5
  445.7 1.6 constant_dynamic-slice_fusion.5
  454.0 1.6 constant_dynamic-slice_fusion.5
  462.3 1.6 constant_dynamic-slice_fusion.5
  470.6 1.6 constant_dynamic-slice_fusion.5
  478.9 1.6 constant_dynamic-slice_fusion.5
  487.3 1.6 constant_dynamic-slice_fusion.5
  495.6 1.6 constant_dynamic-slice_fusion.5
  503.9 1.6 constant_dynamic-slice_fusion.5
  512.2 1.6 constant_dynamic-slice_fusion.5
  520.5 1.6 constant_dynamic-slice_fusion.5
  528.8 1.6 constant_dynamic-slice_fusion.5
  537.1 1.6 constant_dynamic-slice_fusion.5
  545.4 1.6 constant_dynamic-slice_fusion.5
  553.8 1.6 constant_dynamic-slice_fusion.5
  562.1 1.6 constant_dynamic-slice_fusion.5
  570.4 1.6 constant_dynamic-slice_fusion.5
  578.7 1.6 constant_dynamic-slice_fusion.5
  587.0 1.6 constant_dynamic-slice_fusion.5
  595.3 1.6 constant_dynamic-slice_fusion.5
  603.6 1.6 constant_dynamic-slice_fusion.5
  611.9 1.6 constant_dynamic-slice_fusion.5
  620.2 1.6 constant_dynamic-slice_fusion.5
  628.6 1.6 constant_dynamic-slice_fusion.5
  636.9 1.6 constant_dynamic-slice_fusion.5
  703.4 1.6 constant_dynamic-slice_fusion.5
  720.0 1.6 constant_dynamic-slice_fusion.5
  736.6 1.6 constant_dynamic-slice_fusion.5
  761.5 1.6 constant_dynamic-slice_fusion.5
  778.2 1.6 constant_dynamic-slice_fusion.5
  869.6 1.6 constant_dynamic-slice_fusion.5
  886.2 1.6 constant_dynamic-slice_fusion.5
  911.2 1.6 constant_dynamic-slice_fusion.5
  927.8 1.6 constant_dynamic-slice_fusion.5
  930.6 48.9 %all_to_all.18 = bf16[20,64,2,384]{3,2,0,1:T(2,128)(2,1)S(1)} all-to-all(bf16[20,64,2,384]{3,2,0,1:T(2,128)(2,1)} %bitcast.45), channel_id=1, replica_groups=mesh['group'=2,'tm'=4,'bl'=2,'pol'=2] {'tm'}, dimensions={1} | all-to-all | bytes 3932160 | tf_op jit(solution)/shard_map/all_to_all | solution.py:73
  979.5 2.8 copy.11
  (1062 shorter events, 336.3 us)
Async XLA Ops:
  0.0 59.7 %copy-start = (f32[2,16,257]{2,1,0:T(8,128)S(1)}, f32[2,16,257]{2,1,0:T(8,128)}, u32[]{:S(2)}) copy-start(f32[2,16,257]{2,1,0:T(8,128)} %param.9) | copy-start | bytes 98692
  26.2 23.1 %copy-start.2 = (bf16[200,64,2,384]{3,2,1,0:T(2,128)(2,1)}, bf16[200,64,2,384]{3,2,1,0:T(2,128)(2,1)S(1)}, u32[]{:S(2)}) copy-start(bf16[200,64,2,384]{3,2,1,0:T(2,128)(2,1)S(1)} %broadcast_multiply_fusion.1) | copy-start | bytes 58982404
  26.2 33.5 %copy-start.3 = (s32[64]{0:T(128)S(1)}, s32[64]{0:T(128)}, u32[]{:S(2)}) copy-start(s32[64]{0:T(128)} %param.8) | copy-start | bytes 772
  49.3 274.3 %collective-permute-start = (bf16[128,64,2,384]{3,2,1,0:T(2,128)(2,1)}, bf16[128,64,2,384]{3,2,1,0:T(2,128)(2,1)}, u32[]{:S(2)}, u32[]{:S(2)}) collective-permute-start(bf16[128,64,2,384]{3,2,1,0:T(2,128)(2,1)} %get-tuple-element.60), channel_id=1, source_target_pairs={{0,4},{4,8},{8,12},{1,5},{5,9},{9,13},{2,6},{6,10},{10,14},{3,7},{... | collective-permute-start | bytes 37748744 | tf_op jit(solution)/shard_map/ppermute | solution.py:15
  52.8 276.5 %collective-permute-start.1 = (bf16[128,64,2,384]{3,2,1,0:T(2,128)(2,1)}, bf16[128,64,2,384]{3,2,1,0:T(2,128)(2,1)}, u32[]{:S(2)}, u32[]{:S(2)}) collective-permute-start(bf16[128,64,2,384]{3,2,1,0:T(2,128)(2,1)} %get-tuple-element.61), channel_id=1, source_target_pairs={{4,0},{8,4},{12,8},{5,1},{9,5},{13,9},{6,2},{10,6},{14,10},{7,3},{... | collective-permute-start | bytes 37748744 | tf_op jit(solution)/shard_map/ppermute | solution.py:18
  930.6 51.7 %copy-start.1 = (f32[2,16,257]{2,1,0:T(8,128)S(1)}, f32[2,16,257]{2,1,0:T(8,128)}, u32[]{:S(2)}) copy-start(f32[2,16,257]{2,1,0:T(8,128)} %param.9) | copy-start | bytes 98692
where the time goes:
time: 990 us; the launch traced here: 982 us
  local copies, waits for them, and re-layouts  373 us (38%)
  waiting for transfers between devices  269 us (27%)
  loops' own time  136 us (14%)
  other arithmetic  115 us (12%)
  blocking collectives  48.9 us (5%)
  matrix products  28.9 us (3%)
  starting transfers between devices  10.4 us (1%)
    ppermute x1, waiting for transfers between devices, padded(): lax.ppermute(lax.slice_in_dim(block, block.shape[dim] - width, None, axis...  264 us
    another operation x1, loops' own time, per_device(): lax.map(per_base, jnp.arange(visibilities.shape[1], dtype=jnp.int32))  136 us
    dynamic_slice x64, local copies, waits for them, and re-layouts, per_base(): lax.dynamic_index_in_dim(extended, base_index, 1, False).astype(jnp.float32)  102 us
    another operation x128, local copies, waits for them, and re-layouts, make_band(): jnp.tile(period_row, (1, block_rows))[:, :block_rows * row_width]  78.5 us
    reshape x64, local copies, waits for them, and re-layouts, filter_block(): band_rows.reshape(2, block_rows // AVG, AVG, row_width).sum(axis=2)  73.2 us
    concatenate x1, other arithmetic, padded(): block = jnp.concatenate([low, block, high], axis=dim)  69.3 us
    all_to_all x1, blocking collectives, per_device(): lax.all_to_all(averaged, 'tm', split_axis=1, concat_axis=0, tiled=True)  48.9 us
    dynamic_slice x64, local copies, waits for them, and re-layouts, per_device(): lax.map(per_base, jnp.arange(visibilities.shape[1], dtype=jnp.int32))  41.2 us
  transfers between devices with their start and end apart: 2, of which 2 were waited for; matrix products, arithmetic and copies ran while one was open for 0% of the time, Pallas kernels for 0%

commit v1 on v0

v1 whole, which is shorter than its diff:
```python
import functools

import jax
import jax.numpy as jnp
from jax import lax
from jax.experimental import pallas as pl
from jax.experimental.pallas import tpu as pltpu
from jax.sharding import PartitionSpec as P

TAPS = 257
AVG = 10
HALF = TAPS // 2
SIDE = -(-HALF // AVG)
GROUP = 8


def round_up(value, step):
    return -(-value // step) * step


def row_plan(block_rows):
    out_count = block_rows // AVG
    side_rows = round_up(2 * SIDE, 8)
    local_rows = round_up(2 * out_count, 8)
    highest = 2 * (block_rows + HALF + AVG * SIDE)
    lowest = 2 * HALF - AVG * (2 * out_count + side_rows)
    period = round_up(max(highest, 2 * (TAPS + AVG) - lowest), 128)
    return out_count, side_rows, local_rows, period


def averaged_taps(filter_bank, period):
    width = TAPS + AVG - 1
    padded = jnp.pad(filter_bank, ((0, 0), (0, 0), (AVG - 1, AVG - 1)))
    total = padded[:, :, 0:width]
    for shift in range(1, AVG):
        total = total + padded[:, :, shift : shift + width]
    real, imag = total[0] * (1.0 / AVG), total[1] * (1.0 / AVG)
    to_real = jnp.stack([real, -imag], axis=-1).reshape(-1, 2 * width)
    to_imag = jnp.stack([imag, real], axis=-1).reshape(-1, 2 * width)
    to_real = jnp.pad(to_real, ((0, 0), (0, period - 2 * width)))
    to_imag = jnp.pad(to_imag, ((0, 0), (0, period - 2 * width)))
    pair = jnp.stack([to_real, jnp.roll(to_imag, -AVG, axis=1)], axis=1)
    return jnp.tile(pair, (1, 4, 1))


def build_bands(taps_ref, flag_ref, band_ref, block_rows):
    out_count, side_rows, local_rows, period = row_plan(block_rows)
    total_rows = 2 * side_rows + local_rows
    flags = flag_ref[...].astype(jnp.float32)

    def one_filter(f, carry):
        tile = pltpu.roll(taps_ref[f], 0, 1, stride=AVG, stride_axis=0)
        start = 0
        for first, rows in (
            (-2 * SIDE, side_rows),
            (0, local_rows),
            (2 * out_count, side_rows),
        ):
            shifts = [(AVG * (first + row) - 2 * HALF) % period for row in range(0, rows, 8)]
            tiles = [pltpu.roll(tile, shift, 1)[:, : 2 * block_rows] for shift in shifts]
            band = jnp.concatenate(tiles, axis=0) * flags
            high = band.astype(jnp.bfloat16)
            low = (band - high.astype(jnp.float32)).astype(jnp.bfloat16)
            band_ref[f, start : start + rows, :] = high
            band_ref[f, total_rows + start : total_rows + start + rows, :] = low
            start += rows
        return carry

    lax.fori_loop(0, taps_ref.shape[0], one_filter, 0)


def filter_kernel(
    index_ref, taps_ref, flag_ref, vis_ref, left_ref, local_ref, right_ref, band_ref, *, first_base
):
    block_rows, group, _, channels = vis_ref.shape
    out_count, side_rows, local_rows, _ = row_plan(block_rows)
    total_rows = 2 * side_rows + local_rows
    side = 2 * SIDE

    @pl.when(pl.program_id(0) == 0)
    def _():
        build_bands(taps_ref, flag_ref, band_ref, block_rows)

    for i in range(group):
        which = index_ref[first_base + pl.program_id(0) * group + i]
        slab = vis_ref[:, i].reshape(2 * block_rows, channels)
        both = jnp.dot(band_ref[which], slab, preferred_element_type=jnp.float32)
        rows = both[:total_rows] + both[total_rows:]
        left_ref[0, side * i : side * (i + 1), :] = rows[:side]
        local_ref[i] = rows[side_rows : side_rows + 2 * out_count]
        start = side_rows + local_rows
        right_ref[0, side * i : side * (i + 1), :] = rows[start : start + side]


def filter_call(visibilities, flags, kernel_index, taps, first, count, group):
    block_rows, _, _, channels = visibilities.shape
    out_count, side_rows, local_rows, period = row_plan(block_rows)
    filters = taps.shape[0]
    steps = count // group
    skip = first // group
    side_shape = jax.ShapeDtypeStruct((steps, 2 * SIDE * group, channels), jnp.float32)
    side_spec = pl.BlockSpec((1, 2 * SIDE * group, channels), lambda i, _: (i, 0, 0))
    return pl.pallas_call(
        functools.partial(filter_kernel, first_base=first),
        grid_spec=pltpu.PrefetchScalarGridSpec(
            num_scalar_prefetch=1,
            grid=(steps,),
            in_specs=[
                pl.BlockSpec((filters, 8, period), lambda i, _: (0, 0, 0)),
                pl.BlockSpec((1, 2 * block_rows), lambda i, _: (0, 0)),
                pl.BlockSpec((block_rows, group, 2, channels), lambda i, _: (0, skip + i, 0, 0)),
            ],
            out_specs=[
                side_spec,
                pl.BlockSpec((group, 2 * out_count, channels), lambda i, _: (i, 0, 0)),
                side_spec,
            ],
            scratch_shapes=[
                pltpu.VMEM(
                    (filters, 2 * (2 * side_rows + local_rows), 2 * block_rows), jnp.bfloat16
                )
            ],
        ),
        out_shape=[
            side_shape,
            jax.ShapeDtypeStruct((count, 2 * out_count, channels), jnp.float32),
            side_shape,
        ],
        cost_estimate=pl.CostEstimate(
            flops=count * 2 * 208 * 400 * channels,
            bytes_accessed=count * block_rows * 2 * channels * 4,
            transcendentals=0,
        ),
    )(kernel_index, taps, flags, visibilities)


def finish_kernel(low_ref, local_ref, high_ref, out_ref, sum_ref):
    group, rows, channels = local_ref.shape
    side = 2 * SIDE
    for i in range(group):
        sum_ref[...] = local_ref[i]
        sum_ref[:side] += low_ref[0, side * i : side * (i + 1), :]
        sum_ref[rows - side :] += high_ref[0, side * i : side * (i + 1), :]
        out_ref[:, i] = sum_ref[...].astype(jnp.bfloat16).reshape(rows // 2, 2, channels)


def finish_call(low, local, high, group):
    count, rows, channels = local.shape
    side_spec = pl.BlockSpec((1, 2 * SIDE * group, channels), lambda i: (i, 0, 0))
    return pl.pallas_call(
        finish_kernel,
        grid=(count // group,),
        in_specs=[
            side_spec,
            pl.BlockSpec((group, rows, channels), lambda i: (i, 0, 0)),
            side_spec,
        ],
        out_specs=pl.BlockSpec((rows // 2, group, 2, channels), lambda i: (0, i, 0, 0)),
        out_shape=jax.ShapeDtypeStruct((rows // 2, count, 2, channels), jnp.bfloat16),
        scratch_shapes=[pltpu.VMEM((rows, channels), jnp.float32)],
    )(low, local, high)


def per_device(visibilities, flag_mask, kernel_index, filter_bank):
    block_rows, bases = visibilities.shape[:2]
    period = row_plan(block_rows)[3]
    taps = averaged_taps(filter_bank, period)
    flags = jnp.repeat(flag_mask, 2)[None, :]
    group = GROUP
    while bases % group:
        group //= 2
    chunk_count = 4 if bases % (4 * group) == 0 else 1
    chunk = bases // chunk_count
    count = lax.axis_size("tm")
    forward = [(i, i + 1) for i in range(count - 1)]
    backward = [(j, i) for i, j in forward]
    parts = []
    for c in range(chunk_count):
        to_left, local, to_right = filter_call(
            visibilities, flags, kernel_index, taps, c * chunk, chunk, group
        )
        low = lax.ppermute(to_right, "tm", forward)
        high = lax.ppermute(to_left, "tm", backward)
        parts.append((low, local, high))
    done = [finish_call(low, local, high, group) for low, local, high in parts]
    averaged = jnp.concatenate(done, axis=1)
    return lax.all_to_all(averaged, "tm", split_axis=1, concat_axis=0, tiled=True)


def solution(mesh):
    placed = (
        P(("group", "tm"), ("bl", "pol"), None, None),
        P(("group", "tm")),
        P(("bl", "pol")),
        P(),
    )
    return jax.shard_map(
        per_device,
        mesh=mesh,
        in_specs=placed,
        out_specs=P("group", ("bl", "pol", "tm"), None, None),
        check_vma=False,
    )
```

time: 990 us -> 146 us (0.15)
  the two profiles are of different devices: /device:TPU:10 before, /device:TPU:0 now
where the time goes in v1:
time: 146 us
  blocking collectives  46.8 us (32%)
  Pallas kernels  45.6 us (31%)
  starting transfers between devices  24.7 us (17%)
  waiting for transfers between devices  14.5 us (10%)
  local copies, waits for them, and re-layouts  8.25 us (6%)
  other arithmetic  5.75 us (4%)
    all_to_all x1, blocking collectives, per_device(): lax.all_to_all(averaged, 'tm', split_axis=1, concat_axis=0, tiled=True)  46.8 us
    pallas_call x4, Pallas kernels, filter_call(): pl.pallas_call(functools.partial(filter_kernel, first_base=first), grid_s...  35.9 us
    ppermute x4, starting transfers between devices, per_device(): low = lax.ppermute(to_right, 'tm', forward)  19.5 us
    ppermute x4, waiting for transfers between devices, per_device(): high = lax.ppermute(to_left, 'tm', backward)  14.4 us
    pallas_call x4, Pallas kernels, finish_call(): pl.pallas_call(finish_kernel, grid=(count // group,), in_specs=[side_spec...  9.72 us
    ppermute x4, starting transfers between devices, per_device(): high = lax.ppermute(to_left, 'tm', backward)  5.16 us
    concatenate x1, other arithmetic, per_device(): averaged = jnp.concatenate(done, axis=1)  4.02 us
  transfers between devices with their start and end apart: 8, of which 2 were waited for; matrix products, arithmetic and copies ran while one was open for 0% of the time, Pallas kernels for 24%

profile of v1, /device:TPU:0, one launch (start us, length us, event | category | flops | bytes accessed | tf_op | source)
XLA Modules:
  0.0 145.7 jit_solution(1534808309180190709)
XLA Ops:
  0.0 1.6 %slice_add_fusion = f32[2,16,266]{2,1,0:T(8,128)S(1)} fusion(f32[2,16,257]{2,1,0:T(8,128)} %param.7), kind=kLoop, calls=%fused_computation.7 | loop fusion | flops 76608 | bytes 66944 | tf_op jit(solution)/shard_map/add | solution.py:36
  1.6 0.2 copy.27
  1.8 0.2 reshape.42
  2.1 0.0 copy-done.8
  2.1 0.1 broadcast_in_dim.3
  2.2 0.7 broadcast_in_dim_reshape.3.flag_ref
  2.9 0.2 copy.26
  3.1 0.2 reshape.41
  3.3 0.1 maximum_bitcast_fusion
  3.4 0.1 pad_maximum_fusion.1
  3.4 0.3 copy.28
  3.7 0.2 tile.4
  3.9 1.2 tile.10.taps_ref
  5.1 8.9 %shard_map.52 = (f32[2,208,384]{2,1,0:T(8,128)}, f32[16,40,384]{2,1,0:T(8,128)}, f32[2,208,384]{2,1,0:T(8,128)}) custom-call(s32[64]{0:T(128)} %index_ref.7, f32[16,8,1024]{2,1,0:T(8,128)} %tile.10.taps_ref, s32[1,400]{1,0:T(1,128)} %broadcast_in_dim_reshape.3.flag_ref, bf16[200,64,2,384]{3,2,1,0:T(2,128)(2,1)} %vis_ref.7), custom_call_target="tpu_custom_call" | custom-call | flops 1022361600 | bytes 9830400 | tf_op jit(solution)/shard_map/pallas_call | solution.py:103
  14.0 5.0 %collective-permute-start.6 = (f32[2,208,384]{2,1,0:T(8,128)}, f32[2,208,384]{2,1,0:T(8,128)S(1)}, u32[]{:S(2)}, u32[]{:S(2)}) collective-permute-start(f32[2,208,384]{2,1,0:T(8,128)} %get-tuple-element.26), channel_id=1, source_target_pairs={{0,4},{4,8},{8,12},{1,5},{5,9},{9,13},{2,6},{6,10},{10,14},{3,7},{... | collective-permute-start | bytes 1916936 | tf_op jit(solution)/shard_map/ppermute | solution.py:182
  19.0 1.3 collective-permute-start.7
  20.3 9.0 %shard_map.50 = (f32[2,208,384]{2,1,0:T(8,128)}, f32[16,40,384]{2,1,0:T(8,128)}, f32[2,208,384]{2,1,0:T(8,128)}) custom-call(s32[64]{0:T(128)} %index_ref.7, f32[16,8,1024]{2,1,0:T(8,128)} %tile.10.taps_ref, s32[1,400]{1,0:T(1,128)} %broadcast_in_dim_reshape.3.flag_ref, bf16[200,64,2,384]{3,2,1,0:T(2,128)(2,1)} %vis_ref.7), custom_call_target="tpu_custom_call" | custom-call | flops 1022361600 | bytes 9830400 | tf_op jit(solution)/shard_map/pallas_call | solution.py:103
  29.3 4.6 %collective-permute-start.4 = (f32[2,208,384]{2,1,0:T(8,128)}, f32[2,208,384]{2,1,0:T(8,128)S(1)}, u32[]{:S(2)}, u32[]{:S(2)}) collective-permute-start(f32[2,208,384]{2,1,0:T(8,128)} %get-tuple-element.23), channel_id=1, source_target_pairs={{0,4},{4,8},{8,12},{1,5},{5,9},{9,13},{2,6},{6,10},{10,14},{3,7},{... | collective-permute-start | bytes 1916936 | tf_op jit(solution)/shard_map/ppermute | solution.py:182
  33.9 1.3 collective-permute-start.5
  35.2 9.0 %shard_map.48 = (f32[2,208,384]{2,1,0:T(8,128)}, f32[16,40,384]{2,1,0:T(8,128)}, f32[2,208,384]{2,1,0:T(8,128)}) custom-call(s32[64]{0:T(128)} %index_ref.7, f32[16,8,1024]{2,1,0:T(8,128)} %tile.10.taps_ref, s32[1,400]{1,0:T(1,128)} %broadcast_in_dim_reshape.3.flag_ref, bf16[200,64,2,384]{3,2,1,0:T(2,128)(2,1)} %vis_ref.7), custom_call_target="tpu_custom_call" | custom-call | flops 1022361600 | bytes 9830400 | tf_op jit(solution)/shard_map/pallas_call | solution.py:103
  44.2 4.6 %collective-permute-start.2 = (f32[2,208,384]{2,1,0:T(8,128)}, f32[2,208,384]{2,1,0:T(8,128)S(1)}, u32[]{:S(2)}, u32[]{:S(2)}) collective-permute-start(f32[2,208,384]{2,1,0:T(8,128)} %get-tuple-element.20), channel_id=1, source_target_pairs={{0,4},{4,8},{8,12},{1,5},{5,9},{9,13},{2,6},{6,10},{10,14},{3,7},{... | collective-permute-start | bytes 1916936 | tf_op jit(solution)/shard_map/ppermute | solution.py:182
  48.8 9.0 %shard_map.46 = (f32[2,208,384]{2,1,0:T(8,128)}, f32[16,40,384]{2,1,0:T(8,128)}, f32[2,208,384]{2,1,0:T(8,128)}) custom-call(s32[64]{0:T(128)} %index_ref.7, f32[16,8,1024]{2,1,0:T(8,128)} %tile.10.taps_ref, s32[1,400]{1,0:T(1,128)} %broadcast_in_dim_reshape.3.flag_ref, bf16[200,64,2,384]{3,2,1,0:T(2,128)(2,1)} %vis_ref.7), custom_call_target="tpu_custom_call" | custom-call | flops 1022361600 | bytes 9830400 | tf_op jit(solution)/shard_map/pallas_call | solution.py:103
  57.7 0.0 collective-permute-done.6.low_ref
  57.7 1.3 collective-permute-start.3
  59.0 0.0 collective-permute-done.7.high_ref
  59.1 0.0 copy-start.5
  59.1 5.4 %collective-permute-start = (f32[2,208,384]{2,1,0:T(8,128)}, f32[2,208,384]{2,1,0:T(8,128)}, u32[]{:S(2)}, u32[]{:S(2)}) collective-permute-start(f32[2,208,384]{2,1,0:T(8,128)} %get-tuple-element.17), channel_id=1, source_target_pairs={{0,4},{4,8},{8,12},{1,5},{5,9},{9,13},{2,6},{6,10},{10,14},{3,7},{... | collective-permute-start | bytes 1916936 | tf_op jit(solution)/shard_map/ppermute | solution.py:182
  64.5 0.0 collective-permute-done.4.low_ref
  64.5 1.3 collective-permute-start.1
  65.7 0.0 copy-done.3
  65.8 0.0 copy-done.5
  65.8 2.4 %shard_map.53 = bf16[20,16,2,384]{3,2,1,0:T(2,128)(2,1)} custom-call(f32[2,208,384]{2,1,0:T(8,128)} %copy-done.3, f32[16,40,384]{2,1,0:T(8,128)} %get-tuple-element.27.local_ref, f32[2,208,384]{2,1,0:T(8,128)} %copy-done.5), custom_call_target="tpu_custom_call" | custom-call | tf_op jit(solution)/shard_map/pallas_call | solution.py:150
  68.2 0.0 collective-permute-done.5.high_ref
  68.2 0.0 copy-done.6
  68.2 0.8 copy-done.7
  69.0 2.4 %shard_map.51 = bf16[20,16,2,384]{3,2,1,0:T(2,128)(2,1)} custom-call(f32[2,208,384]{2,1,0:T(8,128)} %copy-done.6, f32[16,40,384]{2,1,0:T(8,128)} %get-tuple-element.24.local_ref, f32[2,208,384]{2,1,0:T(8,128)} %copy-done.7), custom_call_target="tpu_custom_call" | custom-call | tf_op jit(solution)/shard_map/pallas_call | solution.py:150
  71.5 0.0 collective-permute-done.2.low_ref
  71.5 5.7 %collective-permute-done.3.high_ref = f32[2,208,384]{2,1,0:T(8,128)} collective-permute-done((f32[2,208,384]{2,1,0:T(8,128)}, f32[2,208,384]{2,1,0:T(8,128)}, u32[]{:S(2)}, u32[]{:S(2)}) %collective-permute-start.3) | collective-permute-done | bytes 639008 | tf_op jit(solution)/shard_map/ppermute | solution.py:183
  77.2 2.4 %shard_map.49 = bf16[20,16,2,384]{3,2,1,0:T(2,128)(2,1)} custom-call(f32[2,208,384]{2,1,0:T(8,128)} %copy-done.4, f32[16,40,384]{2,1,0:T(8,128)} %get-tuple-element.21.local_ref, f32[2,208,384]{2,1,0:T(8,128)} %collective-permute-done.3.high_ref), custom_call_target="tpu_custom_call" | custom-call | tf_op jit(solution)/shard_map/pallas_call | solution.py:150
  79.6 0.0 collective-permute-done.low_ref
  79.7 8.7 %collective-permute-done.1.high_ref = f32[2,208,384]{2,1,0:T(8,128)} collective-permute-done((f32[2,208,384]{2,1,0:T(8,128)}, f32[2,208,384]{2,1,0:T(8,128)}, u32[]{:S(2)}, u32[]{:S(2)}) %collective-permute-start.1) | collective-permute-done | bytes 639008 | tf_op jit(solution)/shard_map/ppermute | solution.py:183
  88.4 2.4 %shard_map.47 = bf16[20,16,2,384]{3,2,1,0:T(2,128)(2,1)} custom-call(f32[2,208,384]{2,1,0:T(8,128)} %collective-permute-done.low_ref, f32[16,40,384]{2,1,0:T(8,128)} %get-tuple-element.18.local_ref, f32[2,208,384]{2,1,0:T(8,128)} %collective-permute-done.1.high_ref), custom_call_target="tpu_custom_call" | custom-call | tf_op jit(solution)/shard_map/pallas_call | solution.py:150
  90.8 0.0 copy-done
  90.8 0.0 copy-done.2
  90.8 4.0 %pad_maximum_fusion = bf16[20,64,2,384]{3,2,1,0:T(2,128)(2,1)S(1)} fusion(bf16[20,16,2,384]{3,2,1,0:T(2,128)(2,1)S(1)} %copy-done, bf16[20,16,2,384]{3,2,1,0:T(2,128)(2,1)S(1)} %copy-done.1, bf16[20,16,2,384]{3,2,1,0:T(2,128)(2,1)S(1)} %copy-done.2, bf16[20,16,2,384]{3,2,1,0:T(2,128)(2,1)} %shard_map.47), kind=kLoop, calls=%fused_computation | loop fusion | flops 2949120 | bytes 3932160 | tf_op jit(solution)/shard_map/concatenate | solution.py:186
  94.8 1.4 copy.29
  96.2 46.8 %all_to_all.18 = bf16[20,64,2,384]{3,2,0,1:T(2,128)(2,1)S(1)} all-to-all(bf16[20,64,2,384]{3,2,0,1:T(2,128)(2,1)S(1)} %copy.29), channel_id=1, replica_groups=mesh['group'=2,'tm'=4,'bl'=2,'pol'=2] {'tm'}, dimensions={1} | all-to-all | bytes 3932160 | tf_op jit(solution)/shard_map/all_to_all | solution.py:187
  142.9 2.8 %copy.30 = bf16[4,20,16,2,384]{4,3,2,1,0:T(2,128)(2,1)} copy(bf16[4,20,16,2,384]{4,3,1,2,0:T(2,128)(2,1)S(1)} %bitcast.18) | data formatting | bytes 3932160 | tf_op jit(solution)/shard_map/all_to_all | solution.py:187
  (15 shorter events, 0.1 us)
Async XLA Ops:
  0.0 2.1 %copy-start.8 = (s32[200]{0:T(256)S(1)}, s32[200]{0:T(256)}, u32[]{:S(2)}) copy-start(s32[200]{0:T(256)} %param.5) | copy-start | bytes 2404
  14.0 43.7 %collective-permute-start.6 = (f32[2,208,384]{2,1,0:T(8,128)}, f32[2,208,384]{2,1,0:T(8,128)S(1)}, u32[]{:S(2)}, u32[]{:S(2)}) collective-permute-start(f32[2,208,384]{2,1,0:T(8,128)} %get-tuple-element.26), channel_id=1, source_target_pairs={{0,4},{4,8},{8,12},{1,5},{5,9},{9,13},{2,6},{6,10},{10,14},{3,7},{... | collective-permute-start | bytes 1916936 | tf_op jit(solution)/shard_map/ppermute | solution.py:182
  19.0 40.0 %collective-permute-start.7 = (f32[2,208,384]{2,1,0:T(8,128)}, f32[2,208,384]{2,1,0:T(8,128)S(1)}, u32[]{:S(2)}, u32[]{:S(2)}) collective-permute-start(f32[2,208,384]{2,1,0:T(8,128)} %get-tuple-element.28), channel_id=1, source_target_pairs={{4,0},{8,4},{12,8},{5,1},{9,5},{13,9},{6,2},{10,6},{14,10},{7,3},{... | collective-permute-start | bytes 1916936 | tf_op jit(solution)/shard_map/ppermute | solution.py:183
  29.3 35.1 %collective-permute-start.4 = (f32[2,208,384]{2,1,0:T(8,128)}, f32[2,208,384]{2,1,0:T(8,128)S(1)}, u32[]{:S(2)}, u32[]{:S(2)}) collective-permute-start(f32[2,208,384]{2,1,0:T(8,128)} %get-tuple-element.23), channel_id=1, source_target_pairs={{0,4},{4,8},{8,12},{1,5},{5,9},{9,13},{2,6},{6,10},{10,14},{3,7},{... | collective-permute-start | bytes 1916936 | tf_op jit(solution)/shard_map/ppermute | solution.py:182
  33.9 34.3 %collective-permute-start.5 = (f32[2,208,384]{2,1,0:T(8,128)}, f32[2,208,384]{2,1,0:T(8,128)S(1)}, u32[]{:S(2)}, u32[]{:S(2)}) collective-permute-start(f32[2,208,384]{2,1,0:T(8,128)} %get-tuple-element.25), channel_id=1, source_target_pairs={{4,0},{8,4},{12,8},{5,1},{9,5},{13,9},{6,2},{10,6},{14,10},{7,3},{... | collective-permute-start | bytes 1916936 | tf_op jit(solution)/shard_map/ppermute | solution.py:183
  44.2 27.3 %collective-permute-start.2 = (f32[2,208,384]{2,1,0:T(8,128)}, f32[2,208,384]{2,1,0:T(8,128)S(1)}, u32[]{:S(2)}, u32[]{:S(2)}) collective-permute-start(f32[2,208,384]{2,1,0:T(8,128)} %get-tuple-element.20), channel_id=1, source_target_pairs={{0,4},{4,8},{8,12},{1,5},{5,9},{9,13},{2,6},{6,10},{10,14},{3,7},{... | collective-permute-start | bytes 1916936 | tf_op jit(solution)/shard_map/ppermute | solution.py:182
  57.7 8.0 %copy-start.3 = (f32[2,208,384]{2,1,0:T(8,128)}, f32[2,208,384]{2,1,0:T(8,128)S(1)}, u32[]{:S(2)}) copy-start(f32[2,208,384]{2,1,0:T(8,128)S(1)} %collective-permute-done.6.low_ref) | copy-start | bytes 1916932
  57.7 19.5 %collective-permute-start.3 = (f32[2,208,384]{2,1,0:T(8,128)}, f32[2,208,384]{2,1,0:T(8,128)}, u32[]{:S(2)}, u32[]{:S(2)}) collective-permute-start(f32[2,208,384]{2,1,0:T(8,128)} %get-tuple-element.22), channel_id=1, source_target_pairs={{4,0},{8,4},{12,8},{5,1},{9,5},{13,9},{6,2},{10,6},{14,10},{7,3},{... | collective-permute-start | bytes 1916936 | tf_op jit(solution)/shard_map/ppermute | solution.py:183
  59.1 6.7 %copy-start.5 = (f32[2,208,384]{2,1,0:T(8,128)}, f32[2,208,384]{2,1,0:T(8,128)S(1)}, u32[]{:S(2)}) copy-start(f32[2,208,384]{2,1,0:T(8,128)S(1)} %collective-permute-done.7.high_ref) | copy-start | bytes 1916932
  59.1 20.6 %collective-permute-start = (f32[2,208,384]{2,1,0:T(8,128)}, f32[2,208,384]{2,1,0:T(8,128)}, u32[]{:S(2)}, u32[]{:S(2)}) collective-permute-start(f32[2,208,384]{2,1,0:T(8,128)} %get-tuple-element.17), channel_id=1, source_target_pairs={{0,4},{4,8},{8,12},{1,5},{5,9},{9,13},{2,6},{6,10},{10,14},{3,7},{... | collective-permute-start | bytes 1916936 | tf_op jit(solution)/shard_map/ppermute | solution.py:182
  64.5 3.8 %copy-start.6 = (f32[2,208,384]{2,1,0:T(8,128)}, f32[2,208,384]{2,1,0:T(8,128)S(1)}, u32[]{:S(2)}) copy-start(f32[2,208,384]{2,1,0:T(8,128)S(1)} %collective-permute-done.4.low_ref) | copy-start | bytes 1916932
  64.5 23.9 %collective-permute-start.1 = (f32[2,208,384]{2,1,0:T(8,128)}, f32[2,208,384]{2,1,0:T(8,128)}, u32[]{:S(2)}, u32[]{:S(2)}) collective-permute-start(f32[2,208,384]{2,1,0:T(8,128)} %get-tuple-element.19), channel_id=1, source_target_pairs={{4,0},{8,4},{12,8},{5,1},{9,5},{13,9},{6,2},{10,6},{14,10},{7,3},{... | collective-permute-start | bytes 1916936 | tf_op jit(solution)/shard_map/ppermute | solution.py:183
  68.2 0.8 copy-start.7
  71.5 5.7 %copy-start.4 = (f32[2,208,384]{2,1,0:T(8,128)}, f32[2,208,384]{2,1,0:T(8,128)S(1)}, u32[]{:S(2)}) copy-start(f32[2,208,384]{2,1,0:T(8,128)S(1)} %collective-permute-done.2.low_ref) | copy-start | bytes 1916932
  79.6 11.1 %copy-start = (bf16[20,16,2,384]{3,2,1,0:T(2,128)(2,1)S(1)}, bf16[20,16,2,384]{3,2,1,0:T(2,128)(2,1)}, u32[]{:S(2)}) copy-start(bf16[20,16,2,384]{3,2,1,0:T(2,128)(2,1)} %shard_map.53) | copy-start | bytes 1474564
  79.6 11.1 %copy-start.1 = (bf16[20,16,2,384]{3,2,1,0:T(2,128)(2,1)S(1)}, bf16[20,16,2,384]{3,2,1,0:T(2,128)(2,1)}, u32[]{:S(2)}) copy-start(bf16[20,16,2,384]{3,2,1,0:T(2,128)(2,1)} %shard_map.51) | copy-start | bytes 1474564
  79.6 11.1 %copy-start.2 = (bf16[20,16,2,384]{3,2,1,0:T(2,128)(2,1)S(1)}, bf16[20,16,2,384]{3,2,1,0:T(2,128)(2,1)}, u32[]{:S(2)}) copy-start(bf16[20,16,2,384]{3,2,1,0:T(2,128)(2,1)} %shard_map.49) | copy-start | bytes 1474564

commit v2 on v1

v2 whole, which is shorter than its diff:
```python
import functools

import jax
import jax.numpy as jnp
from jax import lax
from jax.experimental import pallas as pl
from jax.experimental.pallas import tpu as pltpu
from jax.sharding import PartitionSpec as P

TAPS = 257
AVG = 10
HALF = TAPS // 2
SIDE = -(-HALF // AVG)
GROUP = 8


def round_up(value, step):
    return -(-value // step) * step


def row_plan(block_rows):
    out_count = block_rows // AVG
    side_rows = round_up(2 * SIDE, 8)
    local_rows = round_up(2 * out_count, 8)
    highest = 2 * (block_rows + HALF + AVG * SIDE)
    lowest = 2 * HALF - AVG * (2 * out_count + side_rows)
    period = round_up(max(highest, 2 * (TAPS + AVG) - lowest), 128)
    return out_count, side_rows, local_rows, period


def averaged_taps(filter_bank, period):
    width = TAPS + AVG - 1
    padded = jnp.pad(filter_bank, ((0, 0), (0, 0), (AVG - 1, AVG - 1)))
    total = padded[:, :, 0:width]
    for shift in range(1, AVG):
        total = total + padded[:, :, shift : shift + width]
    real, imag = total[0] * (1.0 / AVG), total[1] * (1.0 / AVG)
    to_real = jnp.stack([real, -imag], axis=-1).reshape(-1, 2 * width)
    to_imag = jnp.stack([imag, real], axis=-1).reshape(-1, 2 * width)
    to_real = jnp.pad(to_real, ((0, 0), (0, period - 2 * width)))
    to_imag = jnp.pad(to_imag, ((0, 0), (0, period - 2 * width)))
    pair = jnp.stack([to_real, jnp.roll(to_imag, -AVG, axis=1)], axis=1)
    return jnp.tile(pair, (1, 4, 1))


def build_bands(taps_ref, flag_ref, band_ref, block_rows):
    out_count, side_rows, local_rows, period = row_plan(block_rows)
    total_rows = 2 * side_rows + local_rows
    flags = flag_ref[...].astype(jnp.float32)

    def one_filter(f, carry):
        tile = pltpu.roll(taps_ref[f], 0, 1, stride=AVG, stride_axis=0)
        start = 0
        for first, rows in (
            (-2 * SIDE, side_rows),
            (0, local_rows),
            (2 * out_count, side_rows),
        ):
            shifts = [(AVG * (first + row) - 2 * HALF) % period for row in range(0, rows, 8)]
            tiles = [pltpu.roll(tile, shift, 1)[:, : 2 * block_rows] for shift in shifts]
            band = jnp.concatenate(tiles, axis=0) * flags
            high = band.astype(jnp.bfloat16)
            low = (band - high.astype(jnp.float32)).astype(jnp.bfloat16)
            band_ref[f, start : start + rows, :] = high
            band_ref[f, total_rows + start : total_rows + start + rows, :] = low
            start += rows
        return carry

    lax.fori_loop(0, taps_ref.shape[0], one_filter, 0)


def band_kernel(taps_ref, flag_ref, band_ref, *, block_rows):
    build_bands(taps_ref, flag_ref, band_ref, block_rows)


def band_call(taps, flags):
    block_rows = flags.shape[1] // 2
    _, side_rows, local_rows, _ = row_plan(block_rows)
    return pl.pallas_call(
        functools.partial(band_kernel, block_rows=block_rows),
        in_specs=[pl.BlockSpec(memory_space=pltpu.VMEM)] * 2,
        out_specs=pl.BlockSpec(memory_space=pltpu.VMEM),
        out_shape=jax.ShapeDtypeStruct(
            (taps.shape[0], 2 * (2 * side_rows + local_rows), 2 * block_rows), jnp.bfloat16
        ),
    )(taps, flags)


def stream_kernel(
    index_ref,
    band_ref,
    vis_ref,
    out_ref,
    slab_ref,
    to_left,
    to_right,
    from_left,
    from_right,
    local_ref,
    sum_ref,
    done_ref,
    load_sem,
    left_send,
    right_send,
    left_recv,
    right_recv,
    done_send,
    done_recv,
    *,
    count,
):
    me = lax.axis_index("tm")
    _, block_rows, group, _, channels = slab_ref.shape
    chunks = done_ref.shape[0]
    per_owner = chunks // count
    out_count, side_rows, local_rows, _ = row_plan(block_rows)
    total_rows = 2 * side_rows + local_rows
    side = 2 * SIDE
    has_left, has_right = me > 0, me < count - 1

    def chunk_at(step):
        turn = step % count
        owner = (turn % 2) * (count - 1 - turn // 2) + (1 - turn % 2) * (turn // 2)
        return owner, step // count

    def load(step):
        owner, part = chunk_at(step)
        first = (owner * per_owner + part) * group
        slot = step % 2
        return pltpu.make_async_copy(
            vis_ref.at[:, pl.ds(first, group)], slab_ref.at[slot], load_sem.at[slot]
        )

    def remote(source, target, send_sem, recv_sem, device):
        return pltpu.make_async_remote_copy(
            src_ref=source,
            dst_ref=target,
            send_sem=send_sem,
            recv_sem=recv_sem,
            device_id={"tm": device},
            device_id_type=pl.DeviceIdType.MESH,
        )

    def leftward(step):
        return remote(
            to_left.at[step],
            from_right.at[step],
            left_send.at[step],
            right_recv.at[step],
            jnp.maximum(me - 1, 0),
        )

    def rightward(step):
        return remote(
            to_right.at[step],
            from_left.at[step],
            right_send.at[step],
            left_recv.at[step],
            jnp.minimum(me + 1, count - 1),
        )

    def placed(source, part):
        return out_ref.at[pl.ds(source * out_count, out_count), pl.ds(part * group, group)]

    def deliver(step):
        owner, part = chunk_at(step)
        return remote(
            done_ref.at[step], placed(me, part), done_send.at[step], done_recv.at[me, part], owner
        )

    def keep(step):
        _, part = chunk_at(step)
        return pltpu.make_async_copy(done_ref.at[step], placed(me, part), done_send.at[step])

    load(0).start()
    barrier = pltpu.get_barrier_semaphore()
    for offset in range(1, count):
        pl.semaphore_signal(
            barrier,
            inc=1,
            device_id={"tm": lax.rem(me + offset, count)},
            device_id_type=pl.DeviceIdType.MESH,
        )
    pl.semaphore_wait(barrier, count - 1)

    def compute(step, carry):
        @pl.when(step + 1 < chunks)
        def _():
            load(step + 1).start()

        load(step).wait()
        owner, part = chunk_at(step)
        first = (owner * per_owner + part) * group
        slot = step % 2
        for i in range(group):
            which = index_ref[first + i]
            slab = slab_ref[slot, :, i].reshape(2 * block_rows, channels)
            both = jnp.dot(band_ref[which], slab, preferred_element_type=jnp.float32)
            rows = both[:total_rows] + both[total_rows:]
            to_left[step, side * i : side * (i + 1), :] = rows[:side]
            local_ref[step, i] = rows[side_rows : side_rows + 2 * out_count]
            start = side_rows + local_rows
            to_right[step, side * i : side * (i + 1), :] = rows[start : start + side]

        @pl.when(has_left)
        def _():
            leftward(step).start()

        @pl.when(has_right)
        def _():
            rightward(step).start()

        return carry

    lax.fori_loop(0, chunks, compute, 0)

    def finish(step, carry):
        @pl.when(has_left)
        def _():
            rightward(step).wait_recv()

        @pl.when(has_right)
        def _():
            leftward(step).wait_recv()

        for i in range(group):
            sum_ref[...] = local_ref[step, i]

            @pl.when(has_left)
            def _():
                sum_ref[:side] += from_left[step, side * i : side * (i + 1), :]

            @pl.when(has_right)
            def _():
                sum_ref[2 * out_count - side :] += from_right[step, side * i : side * (i + 1), :]

            done_ref[step, :, i] = (
                sum_ref[...].astype(jnp.bfloat16).reshape(out_count, 2, channels)
            )
        owner, _ = chunk_at(step)

        @pl.when(owner == me)
        def _():
            keep(step).start()

        @pl.when(owner != me)
        def _():
            deliver(step).start()

        return carry

    lax.fori_loop(0, chunks, finish, 0)

    def drain(step, carry):
        @pl.when(has_left)
        def _():
            leftward(step).wait_send()

        @pl.when(has_right)
        def _():
            rightward(step).wait_send()

        owner, _ = chunk_at(step)

        @pl.when(owner == me)
        def _():
            keep(step).wait()

        @pl.when(owner != me)
        def _():
            deliver(step).wait_send()

        return carry

    lax.fori_loop(0, chunks, drain, 0)

    def collect(turn, carry):
        source = lax.rem(me + 1 + turn, count)
        for part in range(per_owner):
            remote(
                done_ref.at[0],
                placed(source, part),
                done_send.at[0],
                done_recv.at[source, part],
                source,
            ).wait_recv()
        return carry

    lax.fori_loop(0, count - 1, collect, 0)


def stream_call(kernel_index, bands, visibilities):
    block_rows, bases, _, channels = visibilities.shape
    count = lax.axis_size("tm")
    out_count = block_rows // AVG
    owned = bases // count
    group = GROUP
    while owned % group:
        group //= 2
    chunks = bases // group
    edge = pltpu.VMEM((chunks, 2 * SIDE * group, channels), jnp.float32)
    chunk_sems = pltpu.SemaphoreType.DMA((chunks,))
    return pl.pallas_call(
        functools.partial(stream_kernel, count=count),
        in_specs=[
            pl.BlockSpec(memory_space=pltpu.SMEM),
            pl.BlockSpec(memory_space=pltpu.VMEM),
            pl.BlockSpec(memory_space=pl.ANY),
        ],
        out_specs=pl.BlockSpec(memory_space=pl.ANY),
        out_shape=jax.ShapeDtypeStruct((count * out_count, owned, 2, channels), jnp.bfloat16),
        scratch_shapes=[
            pltpu.VMEM((2, block_rows, group, 2, channels), jnp.bfloat16),
            edge,
            edge,
            edge,
            edge,
            pltpu.VMEM((chunks, group, 2 * out_count, channels), jnp.float32),
            pltpu.VMEM((2 * out_count, channels), jnp.float32),
            pltpu.VMEM((chunks, out_count, group, 2, channels), jnp.bfloat16),
            pltpu.SemaphoreType.DMA((2,)),
            chunk_sems,
            chunk_sems,
            chunk_sems,
            chunk_sems,
            chunk_sems,
            pltpu.SemaphoreType.DMA((count, owned // group)),
        ],
        compiler_params=pltpu.CompilerParams(
            collective_id=0, has_side_effects=True, vmem_limit_bytes=50 * 1024 * 1024
        ),
    )(kernel_index, bands, visibilities)


def per_device(visibilities, flag_mask, kernel_index, filter_bank):
    period = row_plan(visibilities.shape[0])[3]
    taps = averaged_taps(filter_bank, period)
    flags = jnp.repeat(flag_mask, 2)[None, :]
    bands = band_call(taps, flags)
    return stream_call(kernel_index, bands, visibilities)


def solution(mesh):
    placed = (
        P(("group", "tm"), ("bl", "pol"), None, None),
        P(("group", "tm")),
        P(("bl", "pol")),
        P(),
    )
    return jax.shard_map(
        per_device,
        mesh=mesh,
        in_specs=placed,
        out_specs=P("group", ("bl", "pol", "tm"), None, None),
        check_vma=False,
    )
```

time: 146 us -> 118 us (0.81)
  the two profiles are of different devices: /device:TPU:0 before, /device:TPU:10 now
where the time goes in v2:
time: 118 us
  Pallas kernels  110 us (93%)
  local copies, waits for them, and re-layouts  5.2 us (4%)
  other arithmetic  1.72 us (1%)
    pallas_call x1, Pallas kernels, stream_call(): pl.pallas_call(functools.partial(stream_kernel, count=count), in_specs=[p...  104 us
    pallas_call x1, Pallas kernels, band_call(): pl.pallas_call(functools.partial(band_kernel, block_rows=block_rows), in_...  6.07 us

profile of v2, /device:TPU:10, one launch (start us, length us, event | category | flops | bytes accessed | tf_op | source)
XLA Modules:
  0.0 117.5 jit_solution(11252666377324150517)
XLA Ops:
  0.0 1.6 %slice_add_fusion = f32[2,16,266]{2,1,0:T(8,128)S(1)} fusion(f32[2,16,257]{2,1,0:T(8,128)} %param.7), kind=kLoop, calls=%fused_computation.6 | loop fusion | flops 76608 | bytes 66944 | tf_op jit(solution)/shard_map/add | solution.py:36
  1.6 0.8 broadcast_in_dim.3
  2.4 0.7 broadcast_in_dim_reshape.3.flag_ref
  3.1 0.2 copy.20
  3.3 0.2 reshape.41
  3.5 0.2 copy.21
  3.7 0.2 reshape.42
  4.0 0.1 maximum_bitcast_fusion
  4.0 0.1 pad_maximum_fusion
  4.1 0.0 copy-start
  4.1 0.3 copy.22
  4.4 0.2 tile.4
  4.6 1.2 tile.10.taps_ref
  5.8 6.1 %shard_map.46.band_ref = bf16[16,208,400]{2,1,0:T(8,128)(2,1)} custom-call(f32[16,8,1024]{2,1,0:T(8,128)} %tile.10.taps_ref, s32[1,400]{1,0:T(1,128)} %broadcast_in_dim_reshape.3.flag_ref), custom_call_target="tpu_custom_call" | custom-call | tf_op jit(solution)/shard_map/pallas_call | solution.py:79
  11.8 0.0 copy-done
  11.8 104.4 %shard_map.47 = bf16[80,16,2,384]{3,2,1,0:T(2,128)(2,1)S(1)} custom-call(s32[64]{0:T(128)S(1)} %copy-done, bf16[16,208,400]{2,1,0:T(8,128)(2,1)} %shard_map.46.band_ref, bf16[200,64,2,384]{3,2,1,0:T(2,128)(2,1)} %vis_ref.1), custom_call_target="tpu_custom_call" | custom-call | tf_op jit(solution)/shard_map/pallas_call | solution.py:303
  116.2 1.3 %copy.24 = bf16[80,16,2,384]{3,2,1,0:T(2,128)(2,1)} copy(bf16[80,16,2,384]{3,2,1,0:T(2,128)(2,1)S(1)} %shard_map.47) | data formatting | bytes 3932160
  (5 shorter events, 0.1 us)
Async XLA Ops:
  4.1 7.7 %copy-start = (s32[64]{0:T(128)S(1)}, s32[64]{0:T(128)}, u32[]{:S(2)}) copy-start(s32[64]{0:T(128)} %index_ref.1) | copy-start | bytes 772

commit v3 on v2

--- a/solution.py
+++ b/solution.py
@@ -39,8 +39,7 @@
     to_imag = jnp.stack([imag, real], axis=-1).reshape(-1, 2 * width)
     to_real = jnp.pad(to_real, ((0, 0), (0, period - 2 * width)))
     to_imag = jnp.pad(to_imag, ((0, 0), (0, period - 2 * width)))
-    pair = jnp.stack([to_real, jnp.roll(to_imag, -AVG, axis=1)], axis=1)
-    return jnp.tile(pair, (1, 4, 1))
+    return jnp.stack([to_real, jnp.roll(to_imag, -AVG, axis=1)], axis=1)
 
 
 def build_bands(taps_ref, flag_ref, band_ref, block_rows):
@@ -49,7 +48,8 @@
     flags = flag_ref[...].astype(jnp.float32)
 
     def one_filter(f, carry):
-        tile = pltpu.roll(taps_ref[f], 0, 1, stride=AVG, stride_axis=0)
+        base = jnp.concatenate([taps_ref[f]] * 4, axis=0)
+        tile = pltpu.roll(base, 0, 1, stride=AVG, stride_axis=0)
         start = 0
         for first, rows in (
             (-2 * SIDE, side_rows),
@@ -66,7 +66,7 @@
             start += rows
         return carry
 
-    lax.fori_loop(0, taps_ref.shape[0], one_filter, 0)
+    lax.fori_loop(0, taps_ref.shape[0], one_filter, 0, unroll=4)
 
 
 def band_kernel(taps_ref, flag_ref, band_ref, *, block_rows):

time: 118 us -> 116 us (0.983)
  local copies, waits for them, and re-layouts: 5.2 us -> 3.99 us
    another operation x3 -> x2, local copies, waits for them, and re-layouts: 1.62 us -> 0.12 us  [averaged_taps(): return jnp.stack([to_real, jnp.roll(to_imag, -AVG, axis=1)], axis=1)]
    pallas_call x1, Pallas kernels: 6.07 us -> 4.72 us  [band_call(): pl.pallas_call(functools.partial(band_kernel, block_rows=block_rows), in_...]
where the time goes in v3:
time: 116 us
  Pallas kernels  109 us (94%)
  local copies, waits for them, and re-layouts  3.99 us (3%)
  other arithmetic  2.43 us (2%)
    pallas_call x1, Pallas kernels, stream_call(): pl.pallas_call(functools.partial(stream_kernel, count=count), in_specs=[p...  104 us
    pallas_call x1, Pallas kernels, band_call(): pl.pallas_call(functools.partial(band_kernel, block_rows=block_rows), in_...  4.72 us

profile of v3, /device:TPU:10, one launch (start us, length us, event | category | flops | bytes accessed | tf_op | source)
XLA Modules:
  0.0 115.6 jit_solution(3004132474889912696)
XLA Ops:
  0.0 1.6 %slice_add_fusion = f32[2,16,266]{2,1,0:T(8,128)S(1)} fusion(f32[2,16,257]{2,1,0:T(8,128)} %param.7), kind=kLoop, calls=%fused_computation.5 | loop fusion | flops 76608 | bytes 66944 | tf_op jit(solution)/shard_map/add | solution.py:36
  1.6 0.8 broadcast_in_dim.3
  2.4 0.7 broadcast_in_dim_reshape.3.flag_ref
  3.1 0.0 copy-start
  3.1 0.2 copy.7
  3.3 0.2 reshape.37
  3.5 0.1 copy.8
  3.6 0.1 stack.20
  3.7 0.2 copy.9
  3.9 0.2 reshape.38
  4.1 0.1 copy.10
  4.2 0.1 pad_slice_fusion
  4.3 0.1 pad_maximum_fusion.1
  4.5 0.8 pad_maximum_fusion.taps_ref
  5.2 4.7 %shard_map.46.band_ref = bf16[16,208,400]{2,1,0:T(8,128)(2,1)} custom-call(f32[16,2,1024]{2,1,0:T(2,128)} %pad_maximum_fusion.taps_ref, s32[1,400]{1,0:T(1,128)} %broadcast_in_dim_reshape.3.flag_ref), custom_call_target="tpu_custom_call" | custom-call | tf_op jit(solution)/shard_map/pallas_call | solution.py:79
  10.0 0.0 copy-done
  10.0 104.4 %shard_map.47 = bf16[80,16,2,384]{3,2,1,0:T(2,128)(2,1)S(1)} custom-call(s32[64]{0:T(128)S(1)} %copy-done, bf16[16,208,400]{2,1,0:T(8,128)(2,1)} %shard_map.46.band_ref, bf16[200,64,2,384]{3,2,1,0:T(2,128)(2,1)} %vis_ref.1), custom_call_target="tpu_custom_call" | custom-call | tf_op jit(solution)/shard_map/pallas_call | solution.py:303
  114.4 1.3 %copy.13 = bf16[80,16,2,384]{3,2,1,0:T(2,128)(2,1)} copy(bf16[80,16,2,384]{3,2,1,0:T(2,128)(2,1)S(1)} %shard_map.47) | data formatting | bytes 3932160
  (6 shorter events, 0.1 us)
Async XLA Ops:
  3.1 6.8 %copy-start = (s32[64]{0:T(128)S(1)}, s32[64]{0:T(128)}, u32[]{:S(2)}) copy-start(s32[64]{0:T(128)} %index_ref.1) | copy-start | bytes 772
